TPU v7x, 32 devices: a whole 2x2x4 slice. The times are simulated.
32 devices in a mesh: blk: 16 (over z, y, core), col: 2 (over x).
Axes of the slice: x: 2, y: 2, z: 4, core: 2. Of those that a mesh axis runs over, the one named last changes fastest.
Arguments:
- encodings: bfloat16 [8192, 1024], P(('blk', 'col')), may hold values from -8 to 8
- first_weight: bfloat16 [1024, 512], replicated, may hold values from -0.1875 to 0.1875
- second_weight: bfloat16 [512, 32], replicated, may hold values from -0.25 to 0.25
- inv_scale: float32 [32], replicated, may hold values from 0.2 to 0.8
- outputscale: float32 [1], replicated, may hold values from 0.5 to 2
- noise: float32 [1], replicated, may hold values from 0.2 to 2
- rhs: float32 [32, 8192], P('col', 'blk'), may hold values from -12 to 12
Outputs:
- solution: float32 [32, 8192], P('col', 'blk')
- residual: float32 [32, 8192], P('col', 'blk')
All inputs are finite; a program needn't handle non-finite values.
Results may differ from a plain program's by a relative error of at most 0.0079.
Values sent between devices are 32-bit elements; how exact they have to be, the bound alone decides.
A program may use at most 64 MiB of HBM per device.

v0:
```python
import jax
import jax.numpy as jnp
from jax import lax
from jax.sharding import PartitionSpec as P


def square_sums(residual):
    return lax.psum(jnp.sum(residual * residual, axis=1), "blk")


def split_blocks(values, width):
    count = values.shape[1] // width
    return values.reshape(values.shape[0], count, width).transpose(1, 0, 2)


def on_device(encodings, first_weight, second_weight, inv_scale, outputscale, noise, rhs):
    hidden = jnp.maximum(
        jnp.dot(encodings, first_weight, preferred_element_type=jnp.float32), 0.0
    ).astype(jnp.bfloat16)
    features = (
        jnp.einsum("hf,nh->fn", second_weight, hidden, preferred_element_type=jnp.float32)
        * inv_scale[:, None]
    )
    paired = lax.all_gather(features, "col", axis=1, tiled=True)
    shard_width = features.shape[1]
    row_norms = jnp.sum(paired * paired, axis=0)
    kernel_scale = outputscale[0]
    nugget = noise[0]
    residual = rhs
    norm_now = square_sums(residual)
    moving = lax.all_to_all(rhs, "col", split_axis=1, concat_axis=0, tiled=True)
    initial = jnp.zeros((moving.shape[0], paired.shape[1]), jnp.float32)

    def advance(running, blocks):
        feat_block, dir_block = blocks
        cross = lax.dot_general(
            paired, feat_block, (((0,), (0,)), ((), ())), precision=lax.Precision.HIGHEST
        )
        distance = (
            row_norms[:, None] + jnp.sum(feat_block * feat_block, axis=0)[None, :] - 2.0 * cross
        )
        kernel_tile = kernel_scale * jnp.exp(-0.5 * distance)
        added = lax.dot_general(
            dir_block, kernel_tile, (((1,), (1,)), ((), ())), precision=lax.Precision.HIGHEST
        )
        return (running + added, None)

    images = lax.scan(
        advance,
        initial,
        (
            split_blocks(lax.all_gather(features, "blk", axis=1, tiled=True), shard_width),
            split_blocks(lax.all_gather(moving, "blk", axis=1, tiled=True), shard_width),
        ),
    )[0]
    images = lax.psum_scatter(images, "col", scatter_dimension=0, tiled=True)
    images = images + nugget * rhs
    bent = lax.psum(jnp.sum(rhs * images, axis=1), "blk")
    step_size = norm_now / bent
    solution = step_size[:, None] * rhs
    residual = residual - step_size[:, None] * images
    return (solution, residual)


def solution(mesh):
    placed = (P(("blk", "col"), None), P(), P(), P(), P(), P(), P("col", "blk"))
    return jax.shard_map(
        on_device,
        mesh=mesh,
        in_specs=placed,
        out_specs=(P("col", "blk"), P("col", "blk")),
        check_vma=False,
    )
```

profile of v0, /device:TPU:0, one launch (start us, length us, event | category | flops | bytes accessed | tf_op | source)
XLA Modules:
  0.0 143.1 jit_solution(18136698835859300657)
XLA Ops:
  7.2 1.5 %copy.27 = f32[2,2,8,256]{3,2,0,1:T(8,128)} copy(f32[2,2,8,256]{3,2,1,0:T(8,128)} %bitcast.64) | data formatting | bytes 65536 | tf_op jit(solution)/shard_map/all_to_all | solution.py:31
  8.6 4.4 %all-to-all-start = ((f32[16,2,256]{2,0,1:T(8,128)}), f32[16,2,256]{2,0,1:T(8,128)S(1)}, u32[]{:S(2)}, u32[]{:S(2)}) async-start(f32[16,2,256]{2,0,1:T(8,128)} %bitcast.45), calls=%async_computation | async-start | bytes 65536 | tf_op jit(solution)/shard_map/all_to_all | solution.py:31
  13.0 1.6 %fusion.12 = f32[32,256]{1,0:T(8,128)S(1)} fusion(bf16[512,32]{0,1:T(8,128)(2,1)S(1)} %copy-done.4, bf16[256,1024]{1,0:T(8,128)(2,1)} %param.9, bf16[1024,512]{1,0:T(8,128)(2,1)S(1)} %copy-done, f32[32]{0:T(128)S(1)} %copy-done.5), kind=kOutput, calls=%fused_computation.18 | convolution fusion | flops 277094400 | bytes 1638528 | tf_op jit(solution)/shard_map/hf,nh->fn/dot_general | solution.py:21
  14.6 4.6 %all_gather.10 = f32[32,512]{1,0:T(8,128)S(1)} all-gather(f32[32,256]{1,0:T(8,128)S(1)} %fusion.12), channel_id=1, replica_groups=mesh['blk'=16,'col'=2] {'col'}, dimensions={1}, use_global_device_ids=true | all-gather | bytes 98304 | tf_op jit(solution)/shard_map/all_gather | solution.py:24
  19.2 23.8 %all_gather.11 = f32[32,4096]{1,0:T(8,128)S(1)} all-gather(f32[32,256]{1,0:T(8,128)S(1)} %fusion.12), channel_id=1, replica_groups=mesh['blk'=16,'col'=2] {'blk'}, dimensions={1}, use_global_device_ids=true | all-gather | bytes 557056 | tf_op jit(solution)/shard_map/all_gather | solution.py:52
  43.1 18.9 %all_gather.9 = f32[32,4096]{1,0:T(8,128)S(1)} all-gather(f32[32,256]{1,0:T(8,128)S(1)} %bitcast.65), channel_id=1, replica_groups=mesh['blk'=16,'col'=2] {'blk'}, dimensions={1}, use_global_device_ids=true | all-gather | bytes 557056 | tf_op jit(solution)/shard_map/all_gather | solution.py:53
  62.2 30.2 %while.11 = (s32[]{:T(128)}, f32[32,512]{1,0:T(8,128)S(1)}, f32[16,32,256]{2,0,1:T(8,128)S(1)}, f32[]{:T(128)}, f32[512]{0:T(512)S(1)}, /*index=5*/f32[16,32,256...) while((s32[]{:T(128)}, f32[32,512]{1,0:T(8,128)S(1)}, f32[16,32,256]{2,0,1:T(8,128)S(1)}, ...), condition=%wide.region_5.6_spmd.clone, body=%wide.region_3.5_spmd.clone.sunk | while | flops 101367552 | bytes 1413239 | solution.py:48
  64.1 1.4 fusion.29
  66.0 1.4 fusion.29
  67.9 1.4 fusion.29
  69.7 1.4 fusion.29
  71.6 1.4 fusion.29
  73.5 1.4 fusion.29
  75.4 1.4 fusion.29
  77.3 1.4 fusion.29
  79.2 1.4 fusion.29
  81.1 1.4 fusion.29
  82.9 1.4 fusion.29
  84.8 1.4 fusion.29
  86.7 1.4 fusion.29
  88.6 1.4 fusion.29
  90.5 1.4 fusion.29
  93.6 8.3 %reduce-scatter.2.cloned.1.call-done = f32[16,512]{1,0:T(8,128)} async-done(((f32[32,512]{1,0:T(8,128)}), f32[16,512]{1,0:T(8,128)}) %reduce-scatter.2.cloned.1.call-update) | async-done | bytes 32784 | tf_op jit(solution)/shard_map/reduce_scatter | solution.py:56
  102.9 32.6 %all-reduce = (f32[16]{0:T(128)S(1)}, f32[16]{0:T(128)S(1)}) all-reduce(f32[16]{0:T(128)S(1)} %get-tuple-element.86, f32[16]{0:T(128)S(1)} %get-tuple-element.85), channel_id=1, replica_groups=mesh['blk'=16,'col'=2] {'blk'}, use_global_device_ids=true, to_apply=%region_1.0 | all-reduce | flops 32 | bytes 256 | tf_op jit(solution)/shard_map/psum | solution.py:8
  (71 shorter events, 11.5 us)
Async XLA Ops:
  7.2 5.9 %copy-start = (bf16[1024,512]{1,0:T(8,128)(2,1)S(1)}, bf16[1024,512]{1,0:T(8,128)(2,1)}, u32[]{:S(2)}) copy-start(bf16[1024,512]{1,0:T(8,128)(2,1)} %param.10) | copy-start | bytes 3145732
  8.6 4.4 %copy-start.4 = (bf16[512,32]{0,1:T(8,128)(2,1)S(1)}, bf16[512,32]{0,1:T(8,128)(2,1)}, u32[]{:S(2)}) copy-start(bf16[512,32]{0,1:T(8,128)(2,1)} %param.11) | copy-start | bytes 98308
  8.6 4.4 %copy-start.5 = (f32[32]{0:T(128)S(1)}, f32[32]{0:T(128)}, u32[]{:S(2)}) copy-start(f32[32]{0:T(128)} %param.12) | copy-start | bytes 388
  8.6 34.5 %all-to-all-start = ((f32[16,2,256]{2,0,1:T(8,128)}), f32[16,2,256]{2,0,1:T(8,128)S(1)}, u32[]{:S(2)}, u32[]{:S(2)}) async-start(f32[16,2,256]{2,0,1:T(8,128)} %bitcast.45), calls=%async_computation | async-start | bytes 65536 | tf_op jit(solution)/shard_map/all_to_all | solution.py:31
  13.0 89.0 %reduce-scatter.2.cloned.1.call-start = ((), (), s32[]{:S(2)}) async-start(), calls=%async_computation.2 | async-start | bytes 98304 | tf_op jit(solution)/shard_map/reduce_scatter | solution.py:56
  92.3 0.6 copy-start.1
  92.3 9.6 %copy-start.2 = (f32[16,512]{1,0:T(8,128)S(1)}, f32[16,512]{1,0:T(8,128)}, u32[]{:S(2)}) copy-start(f32[16,512]{1,0:T(8,128)} %param.15) | copy-start | bytes 98308
  102.0 33.6 %copy-start.3 = (f32[16,512]{1,0:T(8,128)S(1)}, f32[16,512]{1,0:T(8,128)}, u32[]{:S(2)}) copy-start(f32[16,512]{1,0:T(8,128)} %reduce-scatter.2.cloned.1.call-done) | copy-start | bytes 98308
Sparse Core Ops, SparseCore 0:
  93.1 8.8 reduce-scatter.1
where the time goes:
time: 144 us; the launch traced here: 143 us
  blocking collectives  79.8 us (55%)
  matrix products  30.1 us (21%)
  between operations  14.7 us (10%)
  waiting for transfers between devices  8.35 us (6%)
  starting transfers between devices  4.37 us (3%)
  local copies, waits for them, and re-layouts  2.89 us (2%)
  other arithmetic  2.1 us (1%)
    psum x1, blocking collectives, square_sums(): return lax.psum(jnp.sum(residual * residual, axis=1), 'blk')  32.6 us
    all_gather x1, blocking collectives, on_device(): lax.all_gather(features, 'blk', axis=1, tiled=True)  23.8 us
    dot_general x16, matrix products, advance(): lax.dot_general(paired, feat_block, (((0,), (0,)), ((), ())), precision=l...  21.9 us
    all_gather x1, blocking collectives, on_device(): lax.all_gather(moving, 'blk', axis=1, tiled=True)  18.9 us
    reduce_scatter x1, waiting for transfers between devices, on_device(): images = lax.psum_scatter(images, 'col', scatter_dimension=0, tiled=True)  8.33 us
    dot_general x16, matrix products, advance(): lax.dot_general(dir_block, kernel_tile, (((1,), (1,)), ((), ())), precisi...  6.59 us
    all_gather x1, blocking collectives, on_device(): paired = lax.all_gather(features, 'col', axis=1, tiled=True)  4.59 us
    all_to_all x1, starting transfers between devices, on_device(): moving = lax.all_to_all(rhs, 'col', split_axis=1, concat_axis=0, tiled=True)  4.37 us
  transfers between devices with their start and end apart: 2, of which 1 were waited for; matrix products, arithmetic and copies ran while one was open for 1% of the time, Pallas kernels for 0%

commit v1 on v0

--- a/solution.py
+++ b/solution.py
@@ -2,6 +2,28 @@
 import jax.numpy as jnp
 from jax import lax
 from jax.sharding import PartitionSpec as P
+
+
+def in_order(blocks, dim):
+    lengths = list(blocks.shape[1:])
+    lengths[dim] *= blocks.shape[0]
+    return jnp.moveaxis(blocks, 0, dim).reshape(lengths)
+
+
+def ring_gather(x, axis, dim):
+    count = lax.axis_size(axis)
+    pairs = [(i, (i + 1) % count) for i in range(count)]
+    back = [(b, a) for a, b in pairs]
+    lower, upper = ([], [])
+    for step in range(count - 1):
+        if step % 2 == 0:
+            lower.append(lax.ppermute(lower[-1] if lower else x, axis, pairs))
+        else:
+            upper.append(lax.ppermute(upper[-1] if upper else x, axis, back))
+    blocks = jnp.stack([*lower[::-1], x, *upper])
+    shift = lax.axis_index(axis) - len(lower)
+    blocks = blocks[(jnp.arange(count) - shift) % count]
+    return in_order(blocks, dim)
 
 
 def square_sums(residual):
@@ -49,7 +71,7 @@
         advance,
         initial,
         (
-            split_blocks(lax.all_gather(features, "blk", axis=1, tiled=True), shard_width),
+            split_blocks(ring_gather(features, "blk", 1), shard_width),
             split_blocks(lax.all_gather(moving, "blk", axis=1, tiled=True), shard_width),
         ),
     )[0]

time: 144 us -> 167 us (1.16)
  starting transfers between devices: 4.37 us -> 30.8 us
  blocking collectives: 79.8 us -> 56.6 us
  waiting for transfers between devices: 8.35 us -> 26.9 us
    ppermute x0 -> x15, starting transfers between devices: none -> 27.5 us  [the longest x7 27 us: ring_gather(): upper.append(lax.ppermute(upper[-1] if upper else x, axis, back))]
    all_gather x1 -> x0, blocking collectives: 23.8 us -> none  [on_device(): lax.all_gather(features, 'blk', axis=1, tiled=True)]
    ppermute x0 -> x15, waiting for transfers between devices: none -> 16 us  [the longest x8 9.82 us: ring_gather(): lower.append(lax.ppermute(lower[-1] if lower else x, axis, pairs))]
    reduce_scatter x1, waiting for transfers between devices: 8.33 us -> 11 us  [on_device(): images = lax.psum_scatter(images, 'col', scatter_dimension=0, tiled=True)]
  transfers between devices with their start and end apart: 2 -> 17, of which waited for: 1 -> 8; matrix products, arithmetic and copies ran while one was open for 1% -> 1% of each run, Pallas kernels for 0% -> 0%
where the time goes in v1:
time: 167 us; the launch traced here: 166 us
  blocking collectives  56.6 us (34%)
  starting transfers between devices  30.8 us (18%)
  matrix products  30.1 us (18%)
  waiting for transfers between devices  26.9 us (16%)
  between operations  14.9 us (9%)
  local copies, waits for them, and re-layouts  3.87 us (2%)
  other arithmetic  2.12 us (1%)
    psum x1, blocking collectives, square_sums(): return lax.psum(jnp.sum(residual * residual, axis=1), 'blk')  32.6 us
    ppermute x7, starting transfers between devices, ring_gather(): upper.append(lax.ppermute(upper[-1] if upper else x, axis, back))  27 us
    dot_general x16, matrix products, advance(): lax.dot_general(paired, feat_block, (((0,), (0,)), ((), ())), precision=l...  21.9 us
    all_gather x1, blocking collectives, on_device(): lax.all_gather(moving, 'blk', axis=1, tiled=True)  19.4 us
    reduce_scatter x1, waiting for transfers between devices, on_device(): images = lax.psum_scatter(images, 'col', scatter_dimension=0, tiled=True)  11 us
    ppermute x8, waiting for transfers between devices, ring_gather(): lower.append(lax.ppermute(lower[-1] if lower else x, axis, pairs))  9.82 us
    dot_general x16, matrix products, advance(): lax.dot_general(dir_block, kernel_tile, (((1,), (1,)), ((), ())), precisi...  6.59 us
    ppermute x7, waiting for transfers between devices, ring_gather(): upper.append(lax.ppermute(upper[-1] if upper else x, axis, back))  6.13 us
  transfers between devices with their start and end apart: 17, of which 8 were waited for; matrix products, arithmetic and copies ran while one was open for 1% of the time, Pallas kernels for 0%

profile of v1, /device:TPU:0, one launch (start us, length us, event | category | flops | bytes accessed | tf_op | source)
XLA Modules:
  0.0 166.1 jit_solution(5288846960889386372)
XLA Ops:
  8.4 1.6 fusion.11
  10.6 6.6 %collective-permute-done = f32[32,256]{1,0:T(8,128)S(1)} collective-permute-done((f32[32,256]{1,0:T(8,128)S(1)}, f32[32,256]{1,0:T(8,128)S(1)}, u32[]{:S(2)}, u32[]{:S(2)}) %collective-permute-start) | collective-permute-done | bytes 32800 | tf_op jit(solution)/shard_map/ppermute | solution.py:20
  17.2 4.4 %collective-permute-start.8 = (f32[32,256]{1,0:T(8,128)S(1)}, f32[32,256]{1,0:T(8,128)S(1)}, u32[]{:S(2)}, u32[]{:S(2)}) collective-permute-start(f32[32,256]{1,0:T(8,128)S(1)} %bitcast.91), channel_id=1, source_target_pairs={{2,0},{4,2},{6,4},{8,6},{10,8},{12,10},{14,12},{16,14},{18,16},{20... | collective-permute-start | bytes 98312 | tf_op jit(solution)/shard_map/ppermute | solution.py:22
  21.6 1.6 collective-permute-done.1
  23.2 4.4 %collective-permute-start.9 = (f32[32,256]{1,0:T(8,128)S(1)}, f32[32,256]{1,0:T(8,128)S(1)}, u32[]{:S(2)}, u32[]{:S(2)}) collective-permute-start(f32[32,256]{1,0:T(8,128)S(1)} %collective-permute-done.8), channel_id=1, source_target_pairs={{2,0},{4,2},{6,4},{8,6},{10,8},{12,10},{14,12},{16,14},{18,16},{20... | collective-permute-start | bytes 98312 | tf_op jit(solution)/shard_map/ppermute | solution.py:22
  27.6 1.6 collective-permute-done.2
  29.9 3.3 %all-to-all-start = ((f32[16,2,256]{2,0,1:T(8,128)}), f32[16,2,256]{2,0,1:T(8,128)S(1)}, u32[]{:S(2)}, u32[]{:S(2)}) async-start(f32[16,2,256]{2,0,1:T(8,128)} %bitcast.72), calls=%async_computation | async-start | bytes 65536 | tf_op jit(solution)/shard_map/all_to_all | solution.py:53
  33.2 4.6 %all_gather.7 = f32[32,512]{1,0:T(8,128)S(1)} all-gather(f32[32,256]{1,0:T(8,128)S(1)} %bitcast.92), channel_id=1, replica_groups=mesh['blk'=16,'col'=2] {'col'}, dimensions={1}, use_global_device_ids=true | all-gather | bytes 98304 | tf_op jit(solution)/shard_map/all_gather | solution.py:46
  37.8 3.5 %collective-permute-start.10 = (f32[32,256]{1,0:T(8,128)S(1)}, f32[32,256]{1,0:T(8,128)S(1)}, u32[]{:S(2)}, u32[]{:S(2)}) collective-permute-start(f32[32,256]{1,0:T(8,128)S(1)} %collective-permute-done.9), channel_id=1, source_target_pairs={{2,0},{4,2},{6,4},{8,6},{10,8},{12,10},{14,12},{16,14},{18,16},{20... | collective-permute-start | bytes 98312 | tf_op jit(solution)/shard_map/ppermute | solution.py:22
  41.3 1.6 collective-permute-done.10
  42.9 4.4 %collective-permute-start.11 = (f32[32,256]{1,0:T(8,128)S(1)}, f32[32,256]{1,0:T(8,128)S(1)}, u32[]{:S(2)}, u32[]{:S(2)}) collective-permute-start(f32[32,256]{1,0:T(8,128)S(1)} %collective-permute-done.10), channel_id=1, source_target_pairs={{2,0},{4,2},{6,4},{8,6},{10,8},{12,10},{14,12},{16,14},{18,16},{20... | collective-permute-start | bytes 98312 | tf_op jit(solution)/shard_map/ppermute | solution.py:22
  47.4 1.6 collective-permute-done.11
  48.9 4.4 %collective-permute-start.12 = (f32[32,256]{1,0:T(8,128)S(1)}, f32[32,256]{1,0:T(8,128)S(1)}, u32[]{:S(2)}, u32[]{:S(2)}) collective-permute-start(f32[32,256]{1,0:T(8,128)S(1)} %collective-permute-done.11), channel_id=1, source_target_pairs={{2,0},{4,2},{6,4},{8,6},{10,8},{12,10},{14,12},{16,14},{18,16},{20... | collective-permute-start | bytes 98312 | tf_op jit(solution)/shard_map/ppermute | solution.py:22
  53.4 1.6 collective-permute-done.12
  55.0 4.4 %collective-permute-start.13 = (f32[32,256]{1,0:T(8,128)S(1)}, f32[32,256]{1,0:T(8,128)S(1)}, u32[]{:S(2)}, u32[]{:S(2)}) collective-permute-start(f32[32,256]{1,0:T(8,128)S(1)} %collective-permute-done.12), channel_id=1, source_target_pairs={{2,0},{4,2},{6,4},{8,6},{10,8},{12,10},{14,12},{16,14},{18,16},{20... | collective-permute-start | bytes 98312 | tf_op jit(solution)/shard_map/ppermute | solution.py:22
  59.5 19.4 %all_gather.6 = f32[32,4096]{1,0:T(8,128)S(1)} all-gather(f32[32,256]{1,0:T(8,128)S(1)} %bitcast.93), channel_id=1, replica_groups=mesh['blk'=16,'col'=2] {'blk'}, dimensions={1}, use_global_device_ids=true | all-gather | bytes 557056 | tf_op jit(solution)/shard_map/all_gather | solution.py:75
  80.5 1.4 collective-permute-done.14
  82.5 30.2 %while.11 = (s32[]{:T(128)}, f32[32,512]{1,0:T(8,128)S(1)}, f32[16,32,256]{2,0,1:T(8,128)S(1)}, f32[]{:T(128)}, f32[512]{0:T(512)S(1)}, /*index=5*/f32[16,32,256...) while((s32[]{:T(128)}, f32[32,512]{1,0:T(8,128)S(1)}, f32[16,32,256]{2,0,1:T(8,128)S(1)}, ...), condition=%wide.region_5.6_spmd.clone, body=%wide.region_3.5_spmd.clone.sunk | while | flops 101367552 | bytes 1413239 | solution.py:70
  82.5 1.4 fusion.30
  90.1 1.4 fusion.30
  101.4 1.4 fusion.30
  108.9 1.4 fusion.30
  114.0 11.0 %reduce-scatter.2.cloned.1.call-done = f32[16,512]{1,0:T(8,128)} async-done(((f32[32,512]{1,0:T(8,128)}), f32[16,512]{1,0:T(8,128)}) %reduce-scatter.2.cloned.1.call-update) | async-done | bytes 32784 | tf_op jit(solution)/shard_map/reduce_scatter | solution.py:78
  125.9 32.6 %all-reduce = (f32[16]{0:T(128)S(1)}, f32[16]{0:T(128)S(1)}) all-reduce(f32[16]{0:T(128)S(1)} %get-tuple-element.86, f32[16]{0:T(128)S(1)} %get-tuple-element.85), channel_id=1, replica_groups=mesh['blk'=16,'col'=2] {'blk'}, use_global_device_ids=true, to_apply=%region_1.0 | all-reduce | flops 32 | bytes 256 | tf_op jit(solution)/shard_map/psum | solution.py:30
  (114 shorter events, 30.9 us)
Async XLA Ops:
  7.2 1.2 copy-start
  7.2 22.1 %copy-start.2 = (f32[16,512]{1,0:T(8,128)S(1)}, f32[16,512]{1,0:T(8,128)}, u32[]{:S(2)}) copy-start(f32[16,512]{1,0:T(8,128)} %param.15) | copy-start | bytes 98308
  10.0 7.1 %collective-permute-start = (f32[32,256]{1,0:T(8,128)S(1)}, f32[32,256]{1,0:T(8,128)S(1)}, u32[]{:S(2)}, u32[]{:S(2)}) collective-permute-start(f32[32,256]{1,0:T(8,128)S(1)} %bitcast.90), channel_id=1, source_target_pairs={{0,2},{2,4},{4,6},{6,8},{8,10},{10,12},{12,14},{14,16},{16,18},{18... | collective-permute-start | bytes 98312 | tf_op jit(solution)/shard_map/ppermute | solution.py:20
  17.2 6.0 %collective-permute-start.1 = (f32[32,256]{1,0:T(8,128)S(1)}, f32[32,256]{1,0:T(8,128)S(1)}, u32[]{:S(2)}, u32[]{:S(2)}) collective-permute-start(f32[32,256]{1,0:T(8,128)S(1)} %collective-permute-done), channel_id=1, source_target_pairs={{0,2},{2,4},{4,6},{6,8},{8,10},{10,12},{12,14},{14,16},{16,18},{18... | collective-permute-start | bytes 98312 | tf_op jit(solution)/shard_map/ppermute | solution.py:20
  17.2 6.1 %collective-permute-start.8 = (f32[32,256]{1,0:T(8,128)S(1)}, f32[32,256]{1,0:T(8,128)S(1)}, u32[]{:S(2)}, u32[]{:S(2)}) collective-permute-start(f32[32,256]{1,0:T(8,128)S(1)} %bitcast.91), channel_id=1, source_target_pairs={{2,0},{4,2},{6,4},{8,6},{10,8},{12,10},{14,12},{16,14},{18,16},{20... | collective-permute-start | bytes 98312 | tf_op jit(solution)/shard_map/ppermute | solution.py:22
  23.2 6.0 %collective-permute-start.2 = (f32[32,256]{1,0:T(8,128)S(1)}, f32[32,256]{1,0:T(8,128)S(1)}, u32[]{:S(2)}, u32[]{:S(2)}) collective-permute-start(f32[32,256]{1,0:T(8,128)S(1)} %collective-permute-done.1), channel_id=1, source_target_pairs={{0,2},{2,4},{4,6},{6,8},{8,10},{10,12},{12,14},{14,16},{16,18},{18... | collective-permute-start | bytes 98312 | tf_op jit(solution)/shard_map/ppermute | solution.py:20
  23.2 14.6 %collective-permute-start.9 = (f32[32,256]{1,0:T(8,128)S(1)}, f32[32,256]{1,0:T(8,128)S(1)}, u32[]{:S(2)}, u32[]{:S(2)}) collective-permute-start(f32[32,256]{1,0:T(8,128)S(1)} %collective-permute-done.8), channel_id=1, source_target_pairs={{2,0},{4,2},{6,4},{8,6},{10,8},{12,10},{14,12},{16,14},{18,16},{20... | collective-permute-start | bytes 98312 | tf_op jit(solution)/shard_map/ppermute | solution.py:22
  29.2 12.1 %collective-permute-start.3 = (f32[32,256]{1,0:T(8,128)S(1)}, f32[32,256]{1,0:T(8,128)S(1)}, u32[]{:S(2)}, u32[]{:S(2)}) collective-permute-start(f32[32,256]{1,0:T(8,128)S(1)} %collective-permute-done.2), channel_id=1, source_target_pairs={{0,2},{2,4},{4,6},{6,8},{8,10},{10,12},{12,14},{14,16},{16,18},{18... | collective-permute-start | bytes 98312 | tf_op jit(solution)/shard_map/ppermute | solution.py:20
  29.9 29.6 %all-to-all-start = ((f32[16,2,256]{2,0,1:T(8,128)}), f32[16,2,256]{2,0,1:T(8,128)S(1)}, u32[]{:S(2)}, u32[]{:S(2)}) async-start(f32[16,2,256]{2,0,1:T(8,128)} %bitcast.72), calls=%async_computation | async-start | bytes 65536 | tf_op jit(solution)/shard_map/all_to_all | solution.py:53
  33.1 91.8 %reduce-scatter.2.cloned.1.call-start = ((), (), s32[]{:S(2)}) async-start(), calls=%async_computation.2 | async-start | bytes 98304 | tf_op jit(solution)/shard_map/reduce_scatter | solution.py:78
  37.8 5.1 %collective-permute-start.10 = (f32[32,256]{1,0:T(8,128)S(1)}, f32[32,256]{1,0:T(8,128)S(1)}, u32[]{:S(2)}, u32[]{:S(2)}) collective-permute-start(f32[32,256]{1,0:T(8,128)S(1)} %collective-permute-done.9), channel_id=1, source_target_pairs={{2,0},{4,2},{6,4},{8,6},{10,8},{12,10},{14,12},{16,14},{18,16},{20... | collective-permute-start | bytes 98312 | tf_op jit(solution)/shard_map/ppermute | solution.py:22
  41.3 6.0 %collective-permute-start.4 = (f32[32,256]{1,0:T(8,128)S(1)}, f32[32,256]{1,0:T(8,128)S(1)}, u32[]{:S(2)}, u32[]{:S(2)}) collective-permute-start(f32[32,256]{1,0:T(8,128)S(1)} %collective-permute-done.3), channel_id=1, source_target_pairs={{0,2},{2,4},{4,6},{6,8},{8,10},{10,12},{12,14},{14,16},{16,18},{18... | collective-permute-start | bytes 98312 | tf_op jit(solution)/shard_map/ppermute | solution.py:20
  42.9 6.0 %collective-permute-start.11 = (f32[32,256]{1,0:T(8,128)S(1)}, f32[32,256]{1,0:T(8,128)S(1)}, u32[]{:S(2)}, u32[]{:S(2)}) collective-permute-start(f32[32,256]{1,0:T(8,128)S(1)} %collective-permute-done.10), channel_id=1, source_target_pairs={{2,0},{4,2},{6,4},{8,6},{10,8},{12,10},{14,12},{16,14},{18,16},{20... | collective-permute-start | bytes 98312 | tf_op jit(solution)/shard_map/ppermute | solution.py:22
  47.4 6.0 %collective-permute-start.5 = (f32[32,256]{1,0:T(8,128)S(1)}, f32[32,256]{1,0:T(8,128)S(1)}, u32[]{:S(2)}, u32[]{:S(2)}) collective-permute-start(f32[32,256]{1,0:T(8,128)S(1)} %collective-permute-done.4), channel_id=1, source_target_pairs={{0,2},{2,4},{4,6},{6,8},{8,10},{10,12},{12,14},{14,16},{16,18},{18... | collective-permute-start | bytes 98312 | tf_op jit(solution)/shard_map/ppermute | solution.py:20
  48.9 6.0 %collective-permute-start.12 = (f32[32,256]{1,0:T(8,128)S(1)}, f32[32,256]{1,0:T(8,128)S(1)}, u32[]{:S(2)}, u32[]{:S(2)}) collective-permute-start(f32[32,256]{1,0:T(8,128)S(1)} %collective-permute-done.11), channel_id=1, source_target_pairs={{2,0},{4,2},{6,4},{8,6},{10,8},{12,10},{14,12},{16,14},{18,16},{20... | collective-permute-start | bytes 98312 | tf_op jit(solution)/shard_map/ppermute | solution.py:22
  53.4 6.1 %collective-permute-start.6 = (f32[32,256]{1,0:T(8,128)S(1)}, f32[32,256]{1,0:T(8,128)S(1)}, u32[]{:S(2)}, u32[]{:S(2)}) collective-permute-start(f32[32,256]{1,0:T(8,128)S(1)} %collective-permute-done.5), channel_id=1, source_target_pairs={{0,2},{2,4},{4,6},{6,8},{8,10},{10,12},{12,14},{14,16},{16,18},{18... | collective-permute-start | bytes 98312 | tf_op jit(solution)/shard_map/ppermute | solution.py:20
  55.0 24.1 %collective-permute-start.13 = (f32[32,256]{1,0:T(8,128)S(1)}, f32[32,256]{1,0:T(8,128)S(1)}, u32[]{:S(2)}, u32[]{:S(2)}) collective-permute-start(f32[32,256]{1,0:T(8,128)S(1)} %collective-permute-done.12), channel_id=1, source_target_pairs={{2,0},{4,2},{6,4},{8,6},{10,8},{12,10},{14,12},{16,14},{18,16},{20... | collective-permute-start | bytes 98312 | tf_op jit(solution)/shard_map/ppermute | solution.py:22
  59.5 20.9 %collective-permute-start.7 = (f32[32,256]{1,0:T(8,128)S(1)}, f32[32,256]{1,0:T(8,128)S(1)}, u32[]{:S(2)}, u32[]{:S(2)}) collective-permute-start(f32[32,256]{1,0:T(8,128)S(1)} %collective-permute-done.6), channel_id=1, source_target_pairs={{0,2},{2,4},{4,6},{6,8},{8,10},{10,12},{12,14},{14,16},{16,18},{18... | collective-permute-start | bytes 98312 | tf_op jit(solution)/shard_map/ppermute | solution.py:20
  79.1 2.8 %collective-permute-start.14 = (f32[32,256]{1,0:T(8,128)S(1)}, f32[32,256]{1,0:T(8,128)S(1)}, u32[]{:S(2)}, u32[]{:S(2)}) collective-permute-start(f32[32,256]{1,0:T(8,128)S(1)} %collective-permute-done.13), channel_id=1, source_target_pairs={{2,0},{4,2},{6,4},{8,6},{10,8},{12,10},{14,12},{16,14},{18,16},{20... | collective-permute-start | bytes 98312 | tf_op jit(solution)/shard_map/ppermute | solution.py:22
  112.7 0.6 copy-start.1
  125.0 33.6 %copy-start.3 = (f32[16,512]{1,0:T(8,128)S(1)}, f32[16,512]{1,0:T(8,128)}, u32[]{:S(2)}) copy-start(f32[16,512]{1,0:T(8,128)} %reduce-scatter.2.cloned.1.call-done) | copy-start | bytes 98308
Sparse Core Ops, SparseCore 0:
  113.5 11.4 reduce-scatter.1
